TPU v7x, 32 devices: a whole 2x2x4 slice. The times are simulated.
32 devices in a mesh: pts: 8 (over z, y), hrs: 4 (over x, core).
Axes of the slice: x: 2, y: 2, z: 4, core: 2. Of those that a mesh axis runs over, the one named last changes fastest.
Arguments:
- fields: float32 [512, 65536], P(('pts', 'hrs')), may hold values from -2000 to 2000, as said below
- probes: float32 [256, 512], replicated, may hold values from -0.25 to 0.25
Outputs:
- basis_rows: float32 [256, 65536], P(None, ('pts', 'hrs'))
- coeffs: float32 [256, 512], replicated
Inputs may be any that keep to these rules, and one draw needn't show every extreme that they name: `fields`: every hour and every grid point carries its own scale, and the values are real-valued and never all zero.
All inputs are finite; a program needn't handle non-finite values.
Results may differ from a plain program's by a relative error of at most 0.00017.
Values sent between devices are 32-bit elements; how exact they have to be, the bound alone decides.
A program may use at most 64 MiB of HBM per device.

v0:
```python
import jax
import jax.numpy as jnp
from jax import lax
from jax.sharding import PartitionSpec as P

highest = lax.Precision.HIGHEST


def contract_last(left, right):
    return lax.dot_general(
        left, right, (((1,), (1,)), ((), ())), precision=highest, preferred_element_type=jnp.float32
    )


def on_device(fields, probes):
    n_pts = lax.axis_size("pts")
    n_hrs = lax.axis_size("hrs")
    panels = lax.all_to_all(fields, ("pts", "hrs"), split_axis=1, concat_axis=0, tiled=True)
    n_points = panels.shape[1] * n_pts * n_hrs
    sketched = jnp.dot(probes, panels, precision=highest, preferred_element_type=jnp.float32)
    cross_sum = lax.psum(contract_last(sketched, panels) / n_points, ("pts", "hrs"))
    local_gram = contract_last(sketched, sketched) / n_points
    gram_sum = lax.psum(local_gram, ("pts", "hrs"))
    factor = jnp.linalg.cholesky(gram_sum)
    basis_rows = lax.linalg.triangular_solve(factor, sketched, left_side=True, lower=True)
    coeffs = lax.linalg.triangular_solve(factor, cross_sum, left_side=True, lower=True)
    return (basis_rows, coeffs)


def solution(mesh):
    return jax.shard_map(
        on_device,
        mesh=mesh,
        in_specs=(P(("pts", "hrs"), None), P()),
        out_specs=(P(None, ("pts", "hrs")), P()),
        check_vma=False,
    )
```

profile of v0, /device:TPU:0, one launch (start us, length us, event | category | flops | bytes accessed | tf_op | source)
XLA Modules:
  0.0 328.4 jit_solution(12238962326394786213)
XLA Ops:
  7.2 0.0 copy-start
  7.2 0.0 all-reduce.4.cloned.1.call-start
  7.2 2.5 copy.17
  9.7 100.7 %all_to_all.19 = f32[16,32,2048]{2,0,1:T(8,128)S(1)} all-to-all(f32[16,32,2048]{2,0,1:T(8,128)S(1)} %bitcast.50), channel_id=1, replica_groups=mesh['pts'=8,'hrs'=4] {'pts','hrs'}, dimensions={1} | all-to-all | bytes 8388608 | tf_op jit(solution)/shard_map/all_to_all | solution.py:18
  110.5 3.7 %fusion.13 = f32[256,2048]{1,0:T(8,128)S(1)} fusion(f32[256,512]{1,0:T(8,128)S(1)} %copy-done, f32[512,2048]{1,0:T(8,128)S(1)} %bitcast.48), kind=kOutput, calls=%fused_computation.38 | convolution fusion | flops 3221225472 | bytes 6815744 | tf_op jit(solution)/shard_map/dot_general | solution.py:20
  114.2 4.5 %convolution_multiply_fusion = f32[256,512]{1,0:T(8,128)} fusion(f32[256,2048]{1,0:T(8,128)S(1)} %fusion.13, f32[512,2048]{1,0:T(8,128)S(1)} %bitcast.49), kind=kOutput, calls=%fused_computation.5 | convolution fusion | flops 3221356544 | bytes 6815744 | tf_op jit(solution)/shard_map/dot_general | solution.py:10
  118.7 2.6 convolution_multiply_fusion.1
  121.3 0.0 all-reduce.4.cloned.1.call-update
  121.3 129.5 %all-reduce.4.cloned.1.call-done = (f32[256,256]{0,1:T(8,128)}, f32[256,512]{1,0:T(8,128)}) async-done(((f32[256,256]{0,1:T(8,128)}, f32[256,512]{1,0:T(8,128)}), (f32[256,256]{0,1:T(8,128)}, f32[256,512]{1,0:T(8,128)})) %all-reduce.4.cloned.1.call-update) | async-done | bytes 786448 | tf_op jit(solution)/shard_map/psum | solution.py:23
  250.9 1.1 copy.13
  252.0 1.0 fusion.4
  253.0 11.9 %cholesky.50 = f32[128,128]{1,0:T(8,128)S(1)} custom-call(f32[128,128]{1,0:T(8,128)S(1)} %cholesky.118), custom_call_target="Cholesky" | custom-call | tf_op jit(solution)/shard_map/jit(cholesky)/cholesky | solution.py:24
  264.9 9.8 %custom-call.16 = f32[1,128,128]{1,2,0:T(8,128)S(1)} custom-call(f32[1,128,128]{2,1,0:T(8,128)S(1)} %get-tuple-element.25), custom_call_target="InvertDiagBlocksLowerTriangular" | custom-call | tf_op jit(solution)/shard_map/jit(cholesky)/cholesky | solution.py:24
  274.7 0.2 constant_dynamic-update-slice_fusion.1
  274.9 0.3 convolution_subtract_fusion.2
  275.2 11.7 %cholesky.105 = f32[128,128]{1,0:T(8,128)S(1)} custom-call(f32[128,128]{1,0:T(8,128)S(1)} %convolution_subtract_fusion.2), custom_call_target="Cholesky" | custom-call | tf_op jit(solution)/shard_map/jit(cholesky)/cholesky | solution.py:24
  287.0 0.6 compare_reduce_fusion
  288.9 0.1 triangular_solve.72
  289.0 4.0 %while.1 = (s32[]{:T(128)}, f32[256,256]{1,0:T(8,128)S(1)}, s32[2,2]{1,0:T(2,128)S(1)}, f32[2,128,128]{2,1,0:T(8,128)S(1)}, s32[]{:T(128)}) while((s32[]{:T(128)}, f32[256,256]{1,0:T(8,128)S(1)}, s32[2,2]{1,0:T(2,128)S(1)}, f32[2,128,128]{2,1,0:T(8,128)S(1)}, s32[]{:T(128)}) %tuple.27), condition=%wide.while_cond, body=%wide.while_body.sunk | while | flops 2 | bytes 131181 | solution.py:25
  289.0 0.6 fusion.27
  289.6 1.4 bitcast_dynamic-update-slice_fusion.2
  291.0 0.6 fusion.27
  291.6 1.4 bitcast_dynamic-update-slice_fusion.2
  293.0 19.9 %custom-call.17 = f32[2,128,128]{1,2,0:T(8,128)S(1)} custom-call(f32[2,128,128]{2,1,0:T(8,128)S(1)} %get-tuple-element.9), custom_call_target="InvertDiagBlocksLowerTriangular" | custom-call | tf_op jit(solution)/shard_map/triangular_solve | solution.py:25
  312.9 1.1 fusion
  314.0 1.4 fusion.2
  315.3 1.3 convolution_subtract_fusion.1
  316.7 0.4 fusion.8
  317.1 0.8 pad_maximum_fusion.1
  317.9 1.0 convolution_subtract_fusion
  319.0 1.0 fusion.9
  320.0 1.5 pad_maximum_fusion
  (10 shorter events, 0.2 us)
Async XLA Ops:
  7.2 103.3 %copy-start = (f32[256,512]{1,0:T(8,128)S(1)}, f32[256,512]{1,0:T(8,128)}, u32[]{:S(2)}) copy-start(f32[256,512]{1,0:T(8,128)} %param.3) | copy-start | bytes 1572868
  7.2 243.7 %all-reduce.4.cloned.1.call-start = ((), (), s32[]{:S(2)}) async-start(), calls=%async_computation.1 | async-start | bytes 1572864 | tf_op jit(solution)/shard_map/psum | solution.py:23
Sparse Core Ops, SparseCore 0:
  121.4 129.3 all-reduce.3
where the time goes:
time: 329 us; the launch traced here: 328 us
  waiting for transfers between devices  130 us (40%)
  blocking collectives  101 us (31%)
  other arithmetic  57.4 us (17%)
  matrix products  17.5 us (5%)
  between operations  15.5 us (5%)
  local copies, waits for them, and re-layouts  7.64 us (2%)
    psum x1, waiting for transfers between devices, on_device(): gram_sum = lax.psum(local_gram, ('pts', 'hrs'))  130 us
    all_to_all x1, blocking collectives, on_device(): lax.all_to_all(fields, ('pts', 'hrs'), split_axis=1, concat_axis=0, tiled...  101 us
    another operation x6, other arithmetic, on_device(): factor = jnp.linalg.cholesky(gram_sum)  34.1 us
    another operation x4, other arithmetic, on_device(): lax.linalg.triangular_solve(factor, sketched, left_side=True, lower=True)  21.5 us
    dot_general x2, matrix products, contract_last(): lax.dot_general(left, right, (((1,), (1,)), ((), ())), precision=highest,...  7.09 us
  transfers between devices with their start and end apart: 1, of which 1 were waited for; matrix products, arithmetic and copies ran while one was open for 0% of the time, Pallas kernels for 0%

commit v1 on v0

--- a/solution.py
+++ b/solution.py
@@ -2,6 +2,7 @@
 import jax.numpy as jnp
 from jax import lax
 from jax.sharding import PartitionSpec as P
+from jax.lax import all_to_all, axis_size
 
 highest = lax.Precision.HIGHEST
 
@@ -15,7 +16,12 @@
 def on_device(fields, probes):
     n_pts = lax.axis_size("pts")
     n_hrs = lax.axis_size("hrs")
-    panels = lax.all_to_all(fields, ("pts", "hrs"), split_axis=1, concat_axis=0, tiled=True)
+    v_next = axis_size(("pts", "hrs"))
+    b_now = jnp.split(fields, v_next, axis=1)
+    res = jnp.stack(b_now)
+    panels = jnp.concatenate(
+        all_to_all(res, axis_name=("pts", "hrs"), split_axis=0, concat_axis=0), axis=0
+    )
     n_points = panels.shape[1] * n_pts * n_hrs
     sketched = jnp.dot(probes, panels, precision=highest, preferred_element_type=jnp.float32)
     cross_sum = lax.psum(contract_last(sketched, panels) / n_points, ("pts", "hrs"))

time: 329 us -> 365 us (1.11)
  local copies, waits for them, and re-layouts: 7.64 us -> 34.5 us
  matrix products: 17.5 us -> 26.7 us
    unnamed x2 -> x33, local copies, waits for them, and re-layouts: 0.01 us -> 28.5 us
    dot_general x2, matrix products: 7.09 us -> 12.1 us  [contract_last(): lax.dot_general(left, right, (((1,), (1,)), ((), ())), precision=highest,...]
where the time goes in v1:
time: 365 us; the launch traced here: 364 us
  waiting for transfers between devices  130 us (36%)
  blocking collectives  101 us (28%)
  other arithmetic  57.2 us (16%)
  local copies, waits for them, and re-layouts  34.5 us (9%)
  matrix products  26.7 us (7%)
  between operations  15.6 us (4%)
    psum x1, waiting for transfers between devices, on_device(): gram_sum = lax.psum(local_gram, ('pts', 'hrs'))  130 us
    all_to_all x1, blocking collectives, on_device(): all_to_all(res, axis_name=('pts', 'hrs'), split_axis=0, concat_axis=0)  101 us
    another operation x6, other arithmetic, on_device(): factor = jnp.linalg.cholesky(gram_sum)  34.2 us
    unnamed x33, local copies, waits for them, and re-layouts  28.5 us
    another operation x4, other arithmetic, on_device(): lax.linalg.triangular_solve(factor, sketched, left_side=True, lower=True)  21.2 us
    dot_general x2, matrix products, contract_last(): lax.dot_general(left, right, (((1,), (1,)), ((), ())), precision=highest,...  12.1 us
  transfers between devices with their start and end apart: 1, of which 1 were waited for; matrix products, arithmetic and copies ran while one was open for 0% of the time, Pallas kernels for 0%

profile of v1, /device:TPU:0, one launch (start us, length us, event | category | flops | bytes accessed | tf_op | source)
XLA Modules:
  0.0 364.5 jit_solution(13375404520502753917)
XLA Ops:
  7.2 1.0 bitcast_dynamic-update-slice_fusion.32
  8.2 0.9 bitcast_dynamic-update-slice_fusion.31
  11.0 0.9 bitcast_dynamic-update-slice_fusion.28
  13.7 0.9 bitcast_dynamic-update-slice_fusion.25
  16.5 0.9 bitcast_dynamic-update-slice_fusion.22
  17.4 0.9 bitcast_dynamic-update-slice_fusion.21
  19.2 0.9 bitcast_dynamic-update-slice_fusion.19
  20.2 0.9 bitcast_dynamic-update-slice_fusion.18
  22.9 0.9 bitcast_dynamic-update-slice_fusion.15
  25.7 0.9 bitcast_dynamic-update-slice_fusion.12
  28.4 0.9 bitcast_dynamic-update-slice_fusion.9
  31.2 0.9 bitcast_dynamic-update-slice_fusion.6
  36.7 100.7 %all_to_all.5 = f32[32,16,2048]{2,1,0:T(8,128)S(1)} all-to-all(f32[32,16,2048]{2,1,0:T(8,128)S(1)} %bitcast_dynamic-update-slice_fusion.1), channel_id=1, replica_groups=mesh['pts'=8,'hrs'=4] {'pts','hrs'}, dimensions={0} | all-to-all | bytes 8388608 | tf_op jit(solution)/shard_map/all_to_all | solution.py:23
  137.5 7.1 %fusion.13 = f32[2048,256]{1,0:T(8,128)S(1)} fusion(f32[512,2048]{1,0:T(8,128)S(1)} %bitcast.109, f32[256,512]{1,0:T(8,128)S(1)} %copy-done), kind=kOutput, calls=%fused_computation.69 | convolution fusion | flops 3221225472 | bytes 6815744 | tf_op jit(solution)/shard_map/dot_general | solution.py:26
  144.6 7.9 %convolution_multiply_fusion = f32[256,512]{1,0:T(8,128)} fusion(f32[2048,256]{1,0:T(8,128)S(1)} %fusion.13, f32[512,2048]{1,0:T(8,128)S(1)} %bitcast.110), kind=kOutput, calls=%fused_computation.4 | convolution fusion | flops 3221356544 | bytes 6815744 | tf_op jit(solution)/shard_map/dot_general | solution.py:11
  152.5 4.2 %convolution_multiply_fusion.1 = f32[256,256]{0,1:T(8,128)} fusion(f32[2048,256]{1,0:T(8,128)S(1)} %fusion.13), kind=kOutput, calls=%fused_computation.6 | convolution fusion | flops 1610678272 | bytes 2359296 | tf_op jit(solution)/shard_map/dot_general | solution.py:11
  156.7 129.5 %all-reduce.4.cloned.1.call-done = (f32[256,256]{0,1:T(8,128)}, f32[256,512]{1,0:T(8,128)}) async-done(((f32[256,256]{0,1:T(8,128)}, f32[256,512]{1,0:T(8,128)}), (f32[256,256]{0,1:T(8,128)}, f32[256,512]{1,0:T(8,128)})) %all-reduce.4.cloned.1.call-update) | async-done | bytes 786448 | tf_op jit(solution)/shard_map/psum | solution.py:29
  286.3 1.1 copy.5
  287.4 1.0 fusion.4
  288.4 11.7 %cholesky.50 = f32[128,128]{1,0:T(8,128)S(1)} custom-call(f32[128,128]{1,0:T(8,128)S(1)} %cholesky.118), custom_call_target="Cholesky" | custom-call | tf_op jit(solution)/shard_map/jit(cholesky)/cholesky | solution.py:30
  300.1 9.8 %custom-call.16 = f32[1,128,128]{1,2,0:T(8,128)S(1)} custom-call(f32[1,128,128]{2,1,0:T(8,128)S(1)} %get-tuple-element.25), custom_call_target="InvertDiagBlocksLowerTriangular" | custom-call | tf_op jit(solution)/shard_map/jit(cholesky)/cholesky | solution.py:30
  310.4 11.9 %cholesky.105 = f32[128,128]{1,0:T(8,128)S(1)} custom-call(f32[128,128]{1,0:T(8,128)S(1)} %convolution_subtract_fusion.2), custom_call_target="Cholesky" | custom-call | tf_op jit(solution)/shard_map/jit(cholesky)/cholesky | solution.py:30
  324.4 4.0 %while.1 = (s32[]{:T(128)}, f32[256,256]{1,0:T(8,128)S(1)}, s32[2,2]{1,0:T(2,128)S(1)}, f32[2,128,128]{2,1,0:T(8,128)S(1)}, s32[]{:T(128)}) while((s32[]{:T(128)}, f32[256,256]{1,0:T(8,128)S(1)}, s32[2,2]{1,0:T(2,128)S(1)}, f32[2,128,128]{2,1,0:T(8,128)S(1)}, s32[]{:T(128)}) %tuple.27), condition=%wide.while_cond, body=%wide.while_body.sunk | while | flops 2 | bytes 131181 | solution.py:31
  325.0 1.4 bitcast_dynamic-update-slice_fusion.34
  327.0 1.4 bitcast_dynamic-update-slice_fusion.34
  328.4 19.7 %custom-call.17 = f32[2,128,128]{1,2,0:T(8,128)S(1)} custom-call(f32[2,128,128]{2,1,0:T(8,128)S(1)} %get-tuple-element.9), custom_call_target="InvertDiagBlocksLowerTriangular" | custom-call | tf_op jit(solution)/shard_map/triangular_solve | solution.py:31
  348.1 1.4 fusion.2
  349.5 1.3 convolution_subtract_fusion.1
  352.1 1.1 fusion
  353.2 1.8 convolution_subtract_fusion
  355.0 1.1 fusion.9
  356.1 1.5 pad_maximum_fusion
  (41 shorter events, 22.2 us)
Async XLA Ops:
  7.2 130.3 %copy-start = (f32[256,512]{1,0:T(8,128)S(1)}, f32[256,512]{1,0:T(8,128)}, u32[]{:S(2)}) copy-start(f32[256,512]{1,0:T(8,128)} %param.3) | copy-start | bytes 1572868
  7.2 279.1 %all-reduce.4.cloned.1.call-start = ((), (), s32[]{:S(2)}) async-start(), calls=%async_computation.1 | async-start | bytes 1572864 | tf_op jit(solution)/shard_map/psum | solution.py:29
Sparse Core Ops, SparseCore 0:
  156.8 129.3 all-reduce.3
